TPU v7x, 32 devices: a whole 2x2x4 slice. The times are simulated.
32 devices in a mesh: dst: 8 (over z, core), src: 4 (over y, x).
Axes of the slice: x: 2, y: 2, z: 4, core: 2. Of those that a mesh axis runs over, the one named last changes fastest.
Arguments:
- features: bfloat16 [256, 3712], P(('dst', 'src')), may hold values from -6 to 6
- edge_source: int32 [8, 2048], P('dst', 'src'), may hold values from 0 to 255, as said below
- edge_target: int32 [8, 2048], P('dst', 'src'), may hold values from 0 to 255, as said below
- edge_valid: int32 [8, 2048], P('dst', 'src'), may hold values from 0 to 1, as said below
- edge_radial: bfloat16 [8, 2048, 128], P('dst', 'src'), may hold values from -6 to 6
- edge_bias: float32 [8, 8, 2048], P('dst', None, 'src'), may hold values from -10 to 330
- w_radial: bfloat16 [128, 128], replicated, may hold values from -0.5 to 0.5
- w_zero: bfloat16 [896, 896], replicated, may hold values from -0.1875 to 0.1875
- w_one_re: bfloat16 [768, 768], replicated, may hold values from -0.15625 to 0.15625
- w_one_im: bfloat16 [768, 768], replicated, may hold values from -0.15625 to 0.15625
- w_two_re: bfloat16 [640, 640], replicated, may hold values from -0.15625 to 0.15625
- w_two_im: bfloat16 [640, 640], replicated, may hold values from -0.15625 to 0.15625
- att_vector: float32 [128], replicated, may hold values from -3 to 3
- w_out: bfloat16 [7, 128, 128], replicated, may hold values from -0.5 to 0.5
Outputs:
- attended: bfloat16 [256, 3712], P(('dst', 'src'))
Inputs may be any that keep to these rules, and one draw needn't show every extreme that they name: `edge_source`: in row d, column block s (the tile of destination block d and source block s) every entry is an atom a with (a // 8) % 4 == s. `edge_target`: in row d every entry lies in [d * 8 * 4, (d + 1) * 8 * 4); every atom is the target of at least one valid slot. `edge_valid`: about five sixteenths of the slots are valid.
All inputs are finite; a program needn't handle non-finite values.
Results may differ from a plain program's by a relative error of at most 0.0093.
Values may be sent and summed in bfloat16 or wider, within the bound.
A program may use at most 128 MiB of HBM per device.

v0:
```python
import jax
import jax.numpy as jnp
import numpy as np
from jax import lax
from jax.sharding import PartitionSpec as P

HEADS = 8
NCOEF = 29
NEG = -1e30


def merged_2(part, axis, combine):
    gathered = jax.tree.map(lambda a: lax.all_gather(a, axis), part)

    def take(source):
        return jax.tree.map(lambda a: lax.dynamic_index_in_dim(a, source, 0, False), gathered)

    return lax.fori_loop(
        1, lax.axis_size(axis), lambda source, state: combine(state, take(source)), take(0)
    )


def product(left, right):
    return jnp.dot(left, right, preferred_element_type=jnp.float32)


def exact_product(left, right):
    return jnp.dot(left, right, precision=lax.Precision.HIGHEST, preferred_element_type=jnp.float32)


def spread_heads(weights, copies, channels):
    return jnp.tile(jnp.repeat(weights, channels // weights.shape[1], axis=1), (1, copies))


def degree_table():
    return np.array(list(range(7)) + list(range(1, 7)) * 2 + list(range(2, 7)) * 2, dtype=np.int32)


def edge_messages(rows, gain, w_zero, w_one_re, w_one_im, w_two_re, w_two_im, att_vector):
    channels = gain.shape[1]
    count = rows.shape[0]

    def part(low, high):
        return (
            rows[:, low * channels : high * channels].astype(jnp.float32)
            * jnp.tile(gain, (1, high - low))
        ).astype(jnp.bfloat16)

    zero = part(0, 7)
    up_one, uq_one = (part(7, 13), part(13, 19))
    up_two, uq_two = (part(19, 24), part(24, 29))
    out_zero = product(zero, w_zero)
    yp_one = product(up_one, w_one_re) - product(uq_one, w_one_im)
    yq_one = product(up_one, w_one_im) + product(uq_one, w_one_re)
    yp_two = product(up_two, w_two_re) - product(uq_two, w_two_im)
    yq_two = product(up_two, w_two_im) + product(uq_two, w_two_re)
    active = jax.nn.silu(out_zero[:, :channels]) * att_vector[None, :]
    logit = active.reshape(count, HEADS, channels // HEADS).sum(axis=2)
    values = jnp.concatenate([out_zero, yp_one, yq_one, yp_two, yq_two], axis=1)
    return (logit, values)


def shards(
    features,
    edge_source,
    edge_target,
    edge_valid,
    edge_radial,
    edge_bias,
    w_radial,
    w_zero,
    w_one_re,
    w_one_im,
    w_two_re,
    w_two_im,
    att_vector,
    w_out,
):
    channels = w_radial.shape[1]
    own_atoms = features.shape[0]
    block_atoms = own_atoms * lax.axis_size("src")
    gathered = lax.all_gather(features, "dst", axis=0, tiled=True)
    source = edge_source[0]
    target = edge_target[0]
    valid = edge_valid[0] > 0
    slots = source.shape[0]
    local_rows = source // block_atoms * own_atoms + source % own_atoms
    rows = jnp.take(gathered, local_rows, axis=0)
    gain = product(edge_radial[0], w_radial)
    logit, values = edge_messages(
        rows, gain, w_zero, w_one_re, w_one_im, w_two_re, w_two_im, att_vector
    )
    logit = logit + edge_bias[0].T
    local_target = target - lax.axis_index("dst") * block_atoms
    member = (
        lax.broadcasted_iota(jnp.int32, (block_atoms, slots), 0) == local_target[None, :]
    ) & valid[None, :]
    one_hot = member.astype(jnp.float32)
    local_top = jnp.max(jnp.where(member[:, :, None], logit[None, :, :], NEG), axis=1)
    edge_top = exact_product(one_hot.T, local_top)
    shifted = jnp.where(valid[:, None], logit - edge_top, 0.0)
    weights = jnp.where(valid[:, None], jnp.exp(shifted), 0.0)
    weighted = values * spread_heads(weights, NCOEF, channels)
    local_den = exact_product(one_hot, weights)
    local_num = exact_product(one_hot, weighted)

    def combine_states(first, second):
        top = jnp.maximum(first[0], second[0])
        scale_first = jnp.exp(first[0] - top)
        scale_second = jnp.exp(second[0] - top)
        den = first[1] * scale_first + second[1] * scale_second
        num = first[2] * spread_heads(scale_first, NCOEF, channels) + second[2] * spread_heads(
            scale_second, NCOEF, channels
        )
        return (top, den, num)

    merged_top, merged_den, merged_num = merged_2(
        (local_top, local_den, local_num), "src", combine_states
    )
    start = lax.axis_index("src") * own_atoms
    own_den = lax.dynamic_slice_in_dim(merged_den, start, own_atoms, 0)
    own_num = lax.dynamic_slice_in_dim(merged_num, start, own_atoms, 0)
    merged = (own_num / spread_heads(own_den, NCOEF, channels)).astype(jnp.bfloat16)
    selected = w_out[degree_table()]
    projected = jnp.einsum(
        "acx,cxy->acy",
        merged.reshape(own_atoms, NCOEF, channels),
        selected,
        preferred_element_type=jnp.float32,
    )
    return projected.astype(jnp.bfloat16).reshape(own_atoms, NCOEF * channels)


def solution(mesh):
    in_specs = (
        P(("dst", "src"), None),
        P("dst", "src"),
        P("dst", "src"),
        P("dst", "src"),
        P("dst", "src", None),
        P("dst", None, "src"),
        P(),
        P(),
        P(),
        P(),
        P(),
        P(),
        P(),
        P(),
    )
    out_specs = P(("dst", "src"), None)
    return jax.shard_map(shards, mesh=mesh, in_specs=in_specs, out_specs=out_specs, check_vma=False)
```

profile of v0, /device:TPU:0, one launch (start us, length us, event | category | flops | bytes accessed | tf_op | source)
XLA Modules:
  0.0 141.0 jit_solution(15630821081774154500)
XLA Ops:
  6.5 1.2 fusion.13
  7.8 0.7 copy-done.10
  8.8 1.7 %copy.53 = f32[512,896]{1,0:T(8,128)} copy(f32[512,896]{0,1:T(8,128)S(1)} %bitcast.111) | data formatting | bytes 3670016 | tf_op jit(solution)/shard_map/tile | solution.py:46
  10.5 16.4 %all_gather.21 = bf16[64,3712]{1,0:T(8,128)(2,1)S(1)} all-gather(bf16[8,3712]{1,0:T(8,128)(2,1)S(1)} %copy-done.16), channel_id=1, replica_groups=mesh['dst'=8,'src'=4] {'dst'}, dimensions={0}, use_global_device_ids=true | all-gather | bytes 534528 | tf_op jit(solution)/shard_map/all_gather | solution.py:82
  27.0 4.3 %gather_fusion.1 = bf16[512,3712]{1,0:T(8,128)(2,1)} fusion(bf16[64,3712]{1,0:T(8,128)(2,1)S(1)} %all_gather.21, s32[1024]{0:T(1024)S(1)} %pad_clamp_fusion), kind=kCustom, calls=%fused_computation.1 | custom fusion | bytes 7604224 | tf_op jit(solution)/shard_map/jit(_take)/gather | solution.py:88
  31.3 2.7 %broadcast_select_fusion = bf16[512,3712]{1,0:T(8,128)(2,1)S(1)} fusion(bf16[512,3712]{1,0:T(8,128)(2,1)} %gather_fusion.1, pred[512]{0:T(512)(128)(4,1)S(1)} %compare_and_fusion), kind=kLoop, calls=%fused_computation.13 | loop fusion | flops 1900544 | bytes 7602688 | tf_op jit(solution)/shard_map/jit(_take)/select_n | solution.py:88
  34.0 2.5 %constant_dynamic-update-slice_fusion = (f32[512,3712]{1,0:T(8,128)}, f32[512,896]{1,0:T(8,128)S(1)}) fusion(bf16[896,896]{1,0:T(8,128)(2,1)S(1)} %copy-done, f32[512,896]{1,0:T(8,128)S(1)} %copy-done.5, bf16[512,3712]{1,0:T(8,128)(2,1)S(1)} %broadcast_select_fusion), kind=kOutput, calls=%fused_computation.46 | convolution fusion | flops 823459840 | bytes 8028160 | tf_op jit(solution)/shard_map/dot_general | solution.py:24
  37.5 1.4 tile.105
  38.8 1.9 %copy.57 = f32[512,768]{1,0:T(8,128)S(1)} copy(f32[512,768]{0,1:T(8,128)} %bitcast.114) | data formatting | bytes 3145728 | tf_op jit(solution)/shard_map/tile | solution.py:46
  40.7 3.6 %fusion.32 = f32[512,768]{1,0:T(8,128)} fusion(bf16[768,768]{1,0:T(8,128)(2,1)} %param.26, f32[512,768]{1,0:T(8,128)S(1)} %copy.57, bf16[512,3712]{1,0:T(8,128)(2,1)} %copy-done.3), kind=kOutput, calls=%fused_computation.80 | convolution fusion | flops 605159424 | bytes 5111808 | tf_op jit(solution)/shard_map/dot_general | solution.py:24
  44.4 3.1 %fusion.31 = f32[512,768]{1,0:T(8,128)} fusion(bf16[768,768]{1,0:T(8,128)(2,1)S(1)} %copy-done.9, f32[512,768]{1,0:T(8,128)S(1)} %copy.57, bf16[512,3712]{1,0:T(8,128)(2,1)} %copy-done.3), kind=kOutput, calls=%fused_computation.79 | convolution fusion | flops 605159424 | bytes 5111808 | tf_op jit(solution)/shard_map/dot_general | solution.py:24
  47.4 1.2 tile.107
  48.7 2.8 %copy.60 = f32[512,640]{1,0:T(8,128)} copy(f32[512,640]{0,1:T(8,128)} %bitcast.115) | data formatting | bytes 2621440 | tf_op jit(solution)/shard_map/tile | solution.py:46
  51.5 3.7 %fusion.30 = f32[512,640]{1,0:T(8,128)} fusion(bf16[640,640]{1,0:T(8,128)(2,1)} %param.28, f32[512,640]{1,0:T(8,128)} %copy.60, bf16[512,3712]{1,0:T(8,128)(2,1)} %copy-done.3), kind=kOutput, calls=%fused_computation.78 | convolution fusion | flops 420413440 | bytes 4096000 | tf_op jit(solution)/shard_map/dot_general | solution.py:24
  55.2 2.9 %fusion.29 = f32[512,640]{1,0:T(8,128)} fusion(bf16[640,640]{1,0:T(8,128)(2,1)S(1)} %copy-done.13, f32[512,640]{1,0:T(8,128)S(1)} %copy-done.1, bf16[512,3712]{1,0:T(8,128)(2,1)} %copy-done.3), kind=kOutput, calls=%fused_computation.77 | convolution fusion | flops 420413440 | bytes 4096000 | tf_op jit(solution)/shard_map/dot_general | solution.py:24
  58.1 4.0 %tile.110 = f32[512,29,128]{0,2,1:T(8,128)} broadcast(f32[512,128]{0,1:T(8,128)S(1)} %bitcast.117), dimensions={0,2} | broadcast | bytes 7864320 | tf_op jit(solution)/shard_map/tile | solution.py:32
  62.2 8.8 %copy.62 = f32[512,3712]{1,0:T(8,128)} copy(f32[512,3712]{0,1:T(8,128)} %bitcast.110) | data formatting | bytes 15204352 | tf_op jit(solution)/shard_map/tile | solution.py:32
  71.0 4.1 %subtract_dynamic-update-slice_fusion = f32[512,3712]{1,0:T(8,128)} fusion(f32[512,3712]{1,0:T(8,128)} %get-tuple-element.202, f32[512,768]{1,0:T(8,128)} %fusion.32, bf16[768,768]{1,0:T(8,128)(2,1)} %param.27, f32[512,768]{1,0:T(8,128)S(1)} %copy.57, bf16[512,3712]{1,0:T(8,128)(2,1)} %copy-done.3), kind=kOutput, calls=%fused_computation.16 | convolution fusion | flops 605552640 | bytes 6684672 | tf_op jit(solution)/shard_map/dot_general | solution.py:24
  75.2 3.5 %add_dynamic-update-slice_fusion = f32[512,3712]{1,0:T(8,128)} fusion(f32[512,3712]{1,0:T(8,128)} %subtract_dynamic-update-slice_fusion, f32[512,768]{1,0:T(8,128)S(1)} %copy-done.6, bf16[768,768]{1,0:T(8,128)(2,1)} %param.26, f32[512,768]{1,0:T(8,128)S(1)} %copy.57, bf16[512,3712]{1,0:T(8,128)(2,1)S(1)} %copy-done.4), kind=kOutput, calls=%fused_computation.15 | convolution fusion | flops 605552640 | bytes 6684672 | tf_op jit(solution)/shard_map/dot_general | solution.py:24
  78.7 1.9 %fusion.6 = f32[512,3712]{1,0:T(8,128)} fusion(f32[512,3712]{1,0:T(8,128)} %add_dynamic-update-slice_fusion, f32[512,640]{1,0:T(8,128)S(1)} %copy-done.8, bf16[640,640]{1,0:T(8,128)(2,1)S(1)} %copy-done.14, f32[512,640]{1,0:T(8,128)S(1)} %copy-done.2, bf16[512,3712]{1,0:T(8,128)(2,1)S(1)} %copy-done.4), kind=kOutput, calls=%fused_computation.22 | convolution fusion | flops 420741120 | bytes 5406720 | tf_op jit(solution)/shard_map/dot_general | solution.py:24
  80.6 1.9 %fusion.5 = f32[512,3712]{1,0:T(8,128)} fusion(f32[512,3712]{1,0:T(8,128)} %fusion.6, f32[512,640]{1,0:T(8,128)S(1)} %copy-done.7, bf16[640,640]{1,0:T(8,128)(2,1)S(1)} %copy-done.15, f32[512,640]{1,0:T(8,128)S(1)} %copy-done.2, bf16[512,3712]{1,0:T(8,128)(2,1)S(1)} %copy-done.4), kind=kOutput, calls=%fused_computation.20 | convolution fusion | flops 420741120 | bytes 5406720 | tf_op jit(solution)/shard_map/dot_general | solution.py:24
  82.6 7.2 %fusion.3 = f32[32,3712]{1,0:T(8,128)} fusion(f32[512,3712]{1,0:T(8,128)} %fusion.5, f32[512,3712]{1,0:T(8,128)S(1)} %bitcast.109, s32[512]{0:T(512)S(1)} %bitcast.121, pred[512]{0:T(512)(128)(4,1)S(1)} %compare_reduce_fusion), kind=kOutput, calls=%fused_computation.11 | convolution fusion | flops 731742208 | bytes 15682048 | tf_op jit(solution)/shard_map/dot_general | solution.py:28
  89.9 1.6 %gather_fusion = bf16[29,128,128]{2,1,0:T(8,128)(2,1)} fusion(bf16[7,128,128]{2,1,0:T(8,128)(2,1)S(1)} %copy-done.12, s32[1024]{0:T(1024)S(1)} %pad_clamp_fusion.1), kind=kCustom, calls=%fused_computation | custom fusion | bytes 1900660 | tf_op jit(solution)/shard_map/gather | solution.py:124
  91.5 8.2 %all-gather.3 = f32[4,32,8]{1,2,0:T(8,128)S(1)} all-gather(f32[1,32,8]{1,2,0:T(8,128)S(1)} %copy.55), channel_id=2, replica_groups=mesh['dst'=8,'src'=4] {'src'}, dimensions={0}, use_global_device_ids=true | all-gather | bytes 5120 | tf_op jit(solution)/shard_map/all_gather | solution.py:13
  99.8 8.4 %all-gather.4 = f32[4,32,8]{1,2,0:T(8,128)S(1)} all-gather(f32[1,32,8]{1,2,0:T(8,128)S(1)} %convolution_bitcast_fusion), channel_id=3, replica_groups=mesh['dst'=8,'src'=4] {'src'}, dimensions={0}, use_global_device_ids=true | all-gather | bytes 5120 | tf_op jit(solution)/shard_map/all_gather | solution.py:13
  108.2 16.4 %all-gather.7.cloned.1.call-done = f32[128,3712]{1,0:T(8,128)} async-done(((f32[32,3712]{1,0:T(8,128)}), f32[128,3712]{1,0:T(8,128)}) %all-gather.7.cloned.1.call-update) | async-done | bytes 1900560 | tf_op jit(solution)/shard_map/all_gather | solution.py:13
  124.7 1.1 slice.44
  125.7 5.9 %while.19 = (s32[]{:T(128)}, f32[32,8]{0,1:T(8,128)S(1)}, f32[32,8]{0,1:T(8,128)S(1)}, f32[32,3712]{1,0:T(8,128)S(1)}, f32[4,32,8]{1,2,0:T(8,128)S(1)}, /*index=...) while((s32[]{:T(128)}, f32[32,8]{0,1:T(8,128)S(1)}, ...), condition=%wide.region_3.4_spmd, body=%wide.region_2.3_spmd.sunk | while | flops 357893 | bytes 3467415 | solution.py:18
  126.0 1.7 %fusion.50 = f32[32,3712]{1,0:T(8,128)S(1)} fusion(f32[4,8,29,128]{3,2,1,0:T(8,128)S(1)} %bitcast.106, f32[32,3712]{1,0:T(8,128)S(1)} %get-tuple-element.268, f32[4,8,29,128]{3,2,1,0:T(8,128)S(1)} %bitcast.107, f32[4,32,3712]{2,1,0:T(8,128)} %get-tuple-element.281, s32[]{:T(128)S(6)} %select_n.137), kind=kLoop, calls=%fused_computation.3.clone.1 | loop fusion | flops 356352 | bytes 2375684 | tf_op jit(solution)/shard_map/while/body/eval_jaxpr/add | solution.py:112
  128.0 1.7 %fusion.50 = f32[32,3712]{1,0:T(8,128)S(1)} fusion(f32[4,8,29,128]{3,2,1,0:T(8,128)S(1)} %bitcast.106, f32[32,3712]{1,0:T(8,128)S(1)} %get-tuple-element.268, f32[4,8,29,128]{3,2,1,0:T(8,128)S(1)} %bitcast.107, f32[4,32,3712]{2,1,0:T(8,128)} %get-tuple-element.281, s32[]{:T(128)S(6)} %select_n.137), kind=kLoop, calls=%fused_computation.3.clone.1 | loop fusion | flops 356352 | bytes 2375684 | tf_op jit(solution)/shard_map/while/body/eval_jaxpr/add | solution.py:112
  130.0 1.7 %fusion.50 = f32[32,3712]{1,0:T(8,128)S(1)} fusion(f32[4,8,29,128]{3,2,1,0:T(8,128)S(1)} %bitcast.106, f32[32,3712]{1,0:T(8,128)S(1)} %get-tuple-element.268, f32[4,8,29,128]{3,2,1,0:T(8,128)S(1)} %bitcast.107, f32[4,32,3712]{2,1,0:T(8,128)} %get-tuple-element.281, s32[]{:T(128)S(6)} %select_n.137), kind=kLoop, calls=%fused_computation.3.clone.1 | loop fusion | flops 356352 | bytes 2375684 | tf_op jit(solution)/shard_map/while/body/eval_jaxpr/add | solution.py:112
  132.0 2.2 %fusion.7 = bf16[8,3712]{1,0:T(8,128)(2,1)} fusion(bf16[29,128,128]{2,1,0:T(8,128)(2,1)} %gather_fusion, f32[32,3712]{1,0:T(8,128)S(1)} %get-tuple-element.182, s32[]{:T(128)S(6)} %select_n.99, f32[8,128]{1,0:T(8,128)S(1)} %tile.112), kind=kOutput, calls=%fused_computation.26 | convolution fusion | flops 7691264 | bytes 1132548 | tf_op jit(solution)/shard_map/acx,cxy->acy/dot_general | solution.py:125
  (96 shorter events, 2.5 us)
Async XLA Ops:
  6.5 27.4 %copy-start = (bf16[896,896]{1,0:T(8,128)(2,1)S(1)}, bf16[896,896]{1,0:T(8,128)(2,1)}, u32[]{:S(2)}) copy-start(bf16[896,896]{1,0:T(8,128)(2,1)} %param.25) | copy-start | bytes 4816900
  6.5 118.1 %all-gather.7.cloned.1.call-start = ((), (), s32[]{:S(2)}) async-start(), calls=%async_computation | async-start | bytes 2375680 | tf_op jit(solution)/shard_map/all_gather | solution.py:13
  7.8 0.7 copy-start.10
  8.7 1.7 %copy-start.16 = (bf16[8,3712]{1,0:T(8,128)(2,1)S(1)}, bf16[8,3712]{1,0:T(8,128)(2,1)}, u32[]{:S(2)}) copy-start(bf16[8,3712]{1,0:T(8,128)(2,1)} %param.18) | copy-start | bytes 178180
  8.8 18.1 %copy-start.18 = (s32[1,512]{1,0:T(1,128)S(1)}, s32[1,512]{1,0:T(1,128)}, u32[]{:S(2)}) copy-start(s32[1,512]{1,0:T(1,128)} %param.19) | copy-start | bytes 6148
  31.3 2.7 %copy-start.5 = (f32[512,896]{1,0:T(8,128)S(1)}, f32[512,896]{1,0:T(8,128)}, u32[]{:S(2)}) copy-start(f32[512,896]{1,0:T(8,128)} %copy.53) | copy-start | bytes 5505028
  34.0 2.6 %copy-start.3 = (bf16[512,3712]{1,0:T(8,128)(2,1)}, bf16[512,3712]{1,0:T(8,128)(2,1)S(1)}, u32[]{:S(2)}) copy-start(bf16[512,3712]{1,0:T(8,128)(2,1)S(1)} %broadcast_select_fusion) | copy-start | bytes 11403268
  34.0 2.6 %copy-start.21 = (f32[128]{0:T(128)S(1)}, f32[128]{0:T(128)}, u32[]{:S(2)}) copy-start(f32[128]{0:T(128)} %param.30) | copy-start | bytes 1540
  34.0 2.8 %copy-start.19 = (s32[1,512]{1,0:T(1,128)S(1)}, s32[1,512]{1,0:T(1,128)}, u32[]{:S(2)}) copy-start(s32[1,512]{1,0:T(1,128)} %param.21) | copy-start | bytes 6148
  34.0 2.8 %copy-start.17 = (f32[1,8,512]{2,1,0:T(8,128)S(1)}, f32[1,8,512]{2,1,0:T(8,128)}, u32[]{:S(2)}) copy-start(f32[1,8,512]{2,1,0:T(8,128)} %param.23) | copy-start | bytes 49156
  34.0 2.9 %copy-start.20 = (s32[1,512]{1,0:T(1,128)S(1)}, s32[1,512]{1,0:T(1,128)}, u32[]{:S(2)}) copy-start(s32[1,512]{1,0:T(1,128)} %param.20) | copy-start | bytes 6148
  36.5 1.0 copy-start.11
  40.7 3.7 %copy-start.9 = (bf16[768,768]{1,0:T(8,128)(2,1)S(1)}, bf16[768,768]{1,0:T(8,128)(2,1)}, u32[]{:S(2)}) copy-start(bf16[768,768]{1,0:T(8,128)(2,1)} %param.27) | copy-start | bytes 3538948
  51.4 3.7 %copy-start.1 = (f32[512,640]{1,0:T(8,128)S(1)}, f32[512,640]{1,0:T(8,128)}, u32[]{:S(2)}) copy-start(f32[512,640]{1,0:T(8,128)} %copy.60) | copy-start | bytes 3932164
  51.4 3.7 %copy-start.13 = (bf16[640,640]{1,0:T(8,128)(2,1)S(1)}, bf16[640,640]{1,0:T(8,128)(2,1)}, u32[]{:S(2)}) copy-start(bf16[640,640]{1,0:T(8,128)(2,1)} %param.29) | copy-start | bytes 2457604
  71.0 4.2 %copy-start.4 = (bf16[512,3712]{1,0:T(8,128)(2,1)S(1)}, bf16[512,3712]{1,0:T(8,128)(2,1)}, u32[]{:S(2)}) copy-start(bf16[512,3712]{1,0:T(8,128)(2,1)} %copy-done.3) | copy-start | bytes 11403268
  71.0 4.2 %copy-start.6 = (f32[512,768]{1,0:T(8,128)S(1)}, f32[512,768]{1,0:T(8,128)}, u32[]{:S(2)}) copy-start(f32[512,768]{1,0:T(8,128)} %fusion.31) | copy-start | bytes 4718596
  71.0 7.7 %copy-start.8 = (f32[512,640]{1,0:T(8,128)S(1)}, f32[512,640]{1,0:T(8,128)}, u32[]{:S(2)}) copy-start(f32[512,640]{1,0:T(8,128)} %fusion.30) | copy-start | bytes 3932164
  75.1 3.5 %copy-start.2 = (f32[512,640]{1,0:T(8,128)S(1)}, f32[512,640]{1,0:T(8,128)}, u32[]{:S(2)}) copy-start(f32[512,640]{1,0:T(8,128)} %copy.60) | copy-start | bytes 3932164
  75.2 3.5 %copy-start.14 = (bf16[640,640]{1,0:T(8,128)(2,1)S(1)}, bf16[640,640]{1,0:T(8,128)(2,1)}, u32[]{:S(2)}) copy-start(bf16[640,640]{1,0:T(8,128)(2,1)} %param.29) | copy-start | bytes 2457604
  75.2 5.4 %copy-start.15 = (bf16[640,640]{1,0:T(8,128)(2,1)S(1)}, bf16[640,640]{1,0:T(8,128)(2,1)}, u32[]{:S(2)}) copy-start(bf16[640,640]{1,0:T(8,128)(2,1)} %param.28) | copy-start | bytes 2457604
  75.2 7.4 %slice-start = ((s8[7602176]{0:T(1024)(128)(4,1)}), s8[4194304]{0:T(1024)(128)(4,1)S(1)}, s32[]{:S(2)}) async-start(s8[7602176]{0:T(1024)(128)(4,1)} %bitcast.108), calls=%async_computation.1 | async-start | bytes 8388608
  78.7 1.9 %copy-start.7 = (f32[512,640]{1,0:T(8,128)S(1)}, f32[512,640]{1,0:T(8,128)}, u32[]{:S(2)}) copy-start(f32[512,640]{1,0:T(8,128)} %fusion.29) | copy-start | bytes 3932164
  78.7 3.8 %slice-start.1 = ((s8[7602176]{0:T(1024)(128)(4,1)}), s8[3407872]{0:T(1024)(128)(4,1)S(1)}, s32[]{:S(2)}) async-start(s8[7602176]{0:T(1024)(128)(4,1)} %bitcast.108), calls=%async_computation.2 | async-start | bytes 6815744
  82.5 7.3 %copy-start.22 = (s32[29]{0:T(128)S(1)}, s32[29]{0:T(128)}, u32[]{:S(2)}) copy-start(s32[29]{0:T(128)} %constant.134) | copy-start | bytes 352
  82.5 7.3 %copy-start.12 = (bf16[7,128,128]{2,1,0:T(8,128)(2,1)S(1)}, bf16[7,128,128]{2,1,0:T(8,128)(2,1)}, u32[]{:S(2)}) copy-start(bf16[7,128,128]{2,1,0:T(8,128)(2,1)} %param.31) | copy-start | bytes 688132
Sparse Core Ops, SparseCore 0:
  89.9 34.7 all-gather.6
where the time goes:
time: 142 us; the launch traced here: 141 us
  matrix products  38.3 us (27%)
  blocking collectives  33 us (23%)
  local copies, waits for them, and re-layouts  31.2 us (22%)
  waiting for transfers between devices  16.5 us (12%)
  between operations  13.7 us (10%)
  other arithmetic  8.12 us (6%)
    dot_general x10, matrix products, product(): return jnp.dot(left, right, preferred_element_type=jnp.float32)  28.6 us
    all_gather x2, blocking collectives, merged_2(): gathered = jax.tree.map(lambda a: lax.all_gather(a, axis), part)  16.6 us
    all_gather x1, waiting for transfers between devices, merged_2(): gathered = jax.tree.map(lambda a: lax.all_gather(a, axis), part)  16.4 us
    all_gather x1, blocking collectives, shards(): gathered = lax.all_gather(features, 'dst', axis=0, tiled=True)  16.4 us
    another operation x15, local copies, waits for them, and re-layouts, spread_heads(): jnp.tile(jnp.repeat(weights, channels // weights.shape[1], axis=1), (1, c...  13.6 us
    another operation x6, local copies, waits for them, and re-layouts, part(): jnp.tile(gain, (1, high - low))  9.16 us
    dot_general x3, matrix products, exact_product(): jnp.dot(left, right, precision=lax.Precision.HIGHEST, preferred_element_t...  7.55 us
    add x3, other arithmetic, combine_states(): first[2] * spread_heads(scale_first, NCOEF, channels)  5.02 us
  transfers between devices with their start and end apart: 1, of which 1 were waited for; matrix products, arithmetic and copies ran while one was open for 1% of the time, Pallas kernels for 0%

commit v1 on v0

--- a/solution.py
+++ b/solution.py
@@ -79,7 +79,9 @@
     channels = w_radial.shape[1]
     own_atoms = features.shape[0]
     block_atoms = own_atoms * lax.axis_size("src")
-    gathered = lax.all_gather(features, "dst", axis=0, tiled=True)
+    gathered = jnp.concatenate(
+        lax.all_to_all(jnp.stack([features] * lax.axis_size("dst")), "dst", 0, 0), axis=0
+    )
     source = edge_source[0]
     target = edge_target[0]
     valid = edge_valid[0] > 0

time: 142 us -> 133 us (0.937)
  blocking collectives: 33 us -> 16.6 us
  starting transfers between devices: 0.01 us -> 6.39 us
  matrix products: 38.3 us -> 34 us
  local copies, waits for them, and re-layouts: 31.2 us -> 34.8 us
  other arithmetic: 8.12 us -> 9.76 us
    all_gather x1 -> x0, blocking collectives: 16.4 us -> none  [shards(): gathered = lax.all_gather(features, 'dst', axis=0, tiled=True)]
    all_to_all x0 -> x1, starting transfers between devices: none -> 6.35 us  [shards(): lax.all_to_all(jnp.stack([features] * lax.axis_size('dst')), 'dst', 0, 0)]
    dot_general x10, matrix products: 28.6 us -> 24.2 us  [product(): return jnp.dot(left, right, preferred_element_type=jnp.float32)]
    another operation x6, local copies, waits for them, and re-layouts: 9.16 us -> 11.2 us  [part(): jnp.tile(gain, (1, high - low))]
    another operation x0 -> x1, local copies, waits for them, and re-layouts: none -> 1.76 us  [shards(): jnp.stack([features] * lax.axis_size('dst'))]
  transfers between devices with their start and end apart: 1 -> 2, of which waited for: 1 -> 2; matrix products, arithmetic and copies ran while one was open for 1% -> 11% of each run, Pallas kernels for 0% -> 0%
where the time goes in v1:
time: 133 us; the launch traced here: 132 us
  local copies, waits for them, and re-layouts  34.8 us (26%)
  matrix products  34 us (26%)
  waiting for transfers between devices  16.8 us (13%)
  blocking collectives  16.6 us (12%)
  between operations  13.8 us (10%)
  other arithmetic  9.76 us (7%)
  starting transfers between devices  6.39 us (5%)
    dot_general x10, matrix products, product(): return jnp.dot(left, right, preferred_element_type=jnp.float32)  24.2 us
    all_gather x2, blocking collectives, merged_2(): gathered = jax.tree.map(lambda a: lax.all_gather(a, axis), part)  16.6 us
    all_gather x1, waiting for transfers between devices, merged_2(): gathered = jax.tree.map(lambda a: lax.all_gather(a, axis), part)  15.6 us
    another operation x15, local copies, waits for them, and re-layouts, spread_heads(): jnp.tile(jnp.repeat(weights, channels // weights.shape[1], axis=1), (1, c...  13.6 us
    another operation x6, local copies, waits for them, and re-layouts, part(): jnp.tile(gain, (1, high - low))  11.2 us
    dot_general x3, matrix products, exact_product(): jnp.dot(left, right, precision=lax.Precision.HIGHEST, preferred_element_t...  7.55 us
    all_to_all x1, starting transfers between devices, shards(): lax.all_to_all(jnp.stack([features] * lax.axis_size('dst')), 'dst', 0, 0)  6.35 us
    add x3, other arithmetic, combine_states(): first[2] * spread_heads(scale_first, NCOEF, channels)  5.02 us
  transfers between devices with their start and end apart: 2, of which 2 were waited for; matrix products, arithmetic and copies ran while one was open for 11% of the time, Pallas kernels for 0%

profile of v1, /device:TPU:0, one launch (start us, length us, event | category | flops | bytes accessed | tf_op | source)
XLA Modules:
  0.0 132.3 jit_solution(14200272617324551065)
XLA Ops:
  6.5 1.8 %stack.2 = bf16[8,8,3712]{2,1,0:T(8,128)(2,1)} broadcast(bf16[8,3712]{1,0:T(8,128)(2,1)} %param.18), dimensions={1,2} | broadcast | bytes 534528 | tf_op jit(solution)/shard_map/stack | solution.py:83
  8.3 6.4 %all-to-all-start = ((bf16[8,8,3712]{2,1,0:T(8,128)(2,1)}), bf16[8,8,3712]{2,1,0:T(8,128)(2,1)S(1)}, u32[]{:S(2)}, u32[]{:S(2)}) async-start(bf16[8,8,3712]{2,1,0:T(8,128)(2,1)} %stack.2), calls=%async_computation | async-start | bytes 950272 | tf_op jit(solution)/shard_map/all_to_all | solution.py:83
  16.4 1.5 %tile.103 = f32[512,7,128]{0,2,1:T(8,128)} broadcast(f32[512,128]{0,1:T(8,128)S(1)} %fusion.13), dimensions={0,2} | broadcast | bytes 2097152 | tf_op jit(solution)/shard_map/tile | solution.py:46
  17.9 2.8 %copy.53 = f32[512,896]{1,0:T(8,128)} copy(f32[512,896]{0,1:T(8,128)} %bitcast.113) | data formatting | bytes 3670016 | tf_op jit(solution)/shard_map/tile | solution.py:46
  20.7 1.4 %tile.105 = f32[512,6,128]{0,2,1:T(8,128)} broadcast(f32[512,128]{0,1:T(8,128)S(1)} %fusion.13), dimensions={0,2} | broadcast | bytes 1835008 | tf_op jit(solution)/shard_map/tile | solution.py:46
  22.1 3.1 %copy.57 = f32[512,768]{1,0:T(8,128)} copy(f32[512,768]{0,1:T(8,128)} %bitcast.116) | data formatting | bytes 3145728 | tf_op jit(solution)/shard_map/tile | solution.py:46
  25.1 1.1 tile.107
  26.3 1.5 %copy.60 = f32[512,640]{1,0:T(8,128)} copy(f32[512,640]{0,1:T(8,128)S(1)} %bitcast.117) | data formatting | bytes 2621440 | tf_op jit(solution)/shard_map/tile | solution.py:46
  27.8 1.1 all-to-all-done
  28.9 4.3 %gather_fusion.1 = bf16[512,3712]{1,0:T(8,128)(2,1)} fusion(bf16[64,3712]{1,0:T(8,128)(2,1)S(1)} %bitcast.107, s32[1024]{0:T(1024)S(1)} %pad_clamp_fusion), kind=kCustom, calls=%fused_computation.1 | custom fusion | bytes 7604224 | tf_op jit(solution)/shard_map/jit(_take)/gather | solution.py:90
  33.2 2.7 %broadcast_select_fusion = bf16[512,3712]{1,0:T(8,128)(2,1)S(1)} fusion(bf16[512,3712]{1,0:T(8,128)(2,1)} %gather_fusion.1, pred[512]{0:T(512)(128)(4,1)S(1)} %compare_and_fusion), kind=kLoop, calls=%fused_computation.13 | loop fusion | flops 1900544 | bytes 7602688 | tf_op jit(solution)/shard_map/jit(_take)/select_n | solution.py:90
  36.0 2.5 %constant_dynamic-update-slice_fusion = (f32[512,3712]{1,0:T(8,128)}, f32[512,896]{1,0:T(8,128)S(1)}) fusion(bf16[896,896]{1,0:T(8,128)(2,1)S(1)} %copy-done, f32[512,896]{1,0:T(8,128)S(1)} %copy-done.7, bf16[512,3712]{1,0:T(8,128)(2,1)S(1)} %broadcast_select_fusion), kind=kOutput, calls=%fused_computation.46 | convolution fusion | flops 823459840 | bytes 8028160 | tf_op jit(solution)/shard_map/dot_general | solution.py:24
  40.8 3.7 %fusion.32 = f32[512,768]{1,0:T(8,128)} fusion(bf16[768,768]{1,0:T(8,128)(2,1)} %param.26, f32[512,768]{1,0:T(8,128)S(1)} %copy-done.1, bf16[512,3712]{1,0:T(8,128)(2,1)} %copy-done.4), kind=kOutput, calls=%fused_computation.80 | convolution fusion | flops 605159424 | bytes 5111808 | tf_op jit(solution)/shard_map/dot_general | solution.py:24
  44.5 1.9 %fusion.31 = f32[512,768]{1,0:T(8,128)} fusion(bf16[768,768]{1,0:T(8,128)(2,1)S(1)} %copy-done.11, f32[512,768]{1,0:T(8,128)S(1)} %copy-done.1, bf16[512,3712]{1,0:T(8,128)(2,1)S(1)} %copy-done.5), kind=kOutput, calls=%fused_computation.79 | convolution fusion | flops 605159424 | bytes 5111808 | tf_op jit(solution)/shard_map/dot_general | solution.py:24
  46.5 1.9 %fusion.30 = f32[512,640]{1,0:T(8,128)} fusion(bf16[640,640]{1,0:T(8,128)(2,1)S(1)} %copy-done.16, f32[512,640]{1,0:T(8,128)S(1)} %copy-done.2, bf16[512,3712]{1,0:T(8,128)(2,1)S(1)} %copy-done.5), kind=kOutput, calls=%fused_computation.78 | convolution fusion | flops 420413440 | bytes 4096000 | tf_op jit(solution)/shard_map/dot_general | solution.py:24
  48.3 1.8 %fusion.29 = f32[512,640]{1,0:T(8,128)} fusion(bf16[640,640]{1,0:T(8,128)(2,1)S(1)} %copy-done.14, f32[512,640]{1,0:T(8,128)S(1)} %copy-done.2, bf16[512,3712]{1,0:T(8,128)(2,1)S(1)} %copy-done.5), kind=kOutput, calls=%fused_computation.77 | convolution fusion | flops 420413440 | bytes 4096000 | tf_op jit(solution)/shard_map/dot_general | solution.py:24
  50.2 4.0 %tile.110 = f32[512,29,128]{0,2,1:T(8,128)} broadcast(f32[512,128]{0,1:T(8,128)S(1)} %bitcast.119), dimensions={0,2} | broadcast | bytes 7864320 | tf_op jit(solution)/shard_map/tile | solution.py:32
  54.2 8.8 %copy.62 = f32[512,3712]{1,0:T(8,128)} copy(f32[512,3712]{0,1:T(8,128)} %bitcast.112) | data formatting | bytes 15204352 | tf_op jit(solution)/shard_map/tile | solution.py:32
  63.1 4.2 %subtract_dynamic-update-slice_fusion = f32[512,3712]{1,0:T(8,128)} fusion(f32[512,3712]{1,0:T(8,128)} %get-tuple-element.202, f32[512,768]{1,0:T(8,128)} %fusion.32, bf16[768,768]{1,0:T(8,128)(2,1)} %param.27, f32[512,768]{1,0:T(8,128)S(1)} %copy-done.1, bf16[512,3712]{1,0:T(8,128)(2,1)} %copy-done.4), kind=kOutput, calls=%fused_computation.16 | convolution fusion | flops 605552640 | bytes 6684672 | tf_op jit(solution)/shard_map/dot_general | solution.py:24
  67.3 3.4 %add_dynamic-update-slice_fusion = f32[512,3712]{1,0:T(8,128)} fusion(f32[512,3712]{1,0:T(8,128)} %subtract_dynamic-update-slice_fusion, f32[512,768]{1,0:T(8,128)S(1)} %copy-done.8, bf16[768,768]{1,0:T(8,128)(2,1)} %param.26, f32[512,768]{1,0:T(8,128)S(1)} %copy-done.1, bf16[512,3712]{1,0:T(8,128)(2,1)S(1)} %copy-done.6), kind=kOutput, calls=%fused_computation.15 | convolution fusion | flops 605552640 | bytes 6684672 | tf_op jit(solution)/shard_map/dot_general | solution.py:24
  70.7 1.9 %fusion.6 = f32[512,3712]{1,0:T(8,128)} fusion(f32[512,3712]{1,0:T(8,128)} %add_dynamic-update-slice_fusion, f32[512,640]{1,0:T(8,128)S(1)} %copy-done.10, bf16[640,640]{1,0:T(8,128)(2,1)S(1)} %copy-done.15, f32[512,640]{1,0:T(8,128)S(1)} %copy-done.3, bf16[512,3712]{1,0:T(8,128)(2,1)S(1)} %copy-done.6), kind=kOutput, calls=%fused_computation.22 | convolution fusion | flops 420741120 | bytes 5406720 | tf_op jit(solution)/shard_map/dot_general | solution.py:24
  72.6 1.9 %fusion.5 = f32[512,3712]{1,0:T(8,128)} fusion(f32[512,3712]{1,0:T(8,128)} %fusion.6, f32[512,640]{1,0:T(8,128)S(1)} %copy-done.9, bf16[640,640]{1,0:T(8,128)(2,1)S(1)} %copy-done.17, f32[512,640]{1,0:T(8,128)S(1)} %copy-done.3, bf16[512,3712]{1,0:T(8,128)(2,1)S(1)} %copy-done.6), kind=kOutput, calls=%fused_computation.20 | convolution fusion | flops 420741120 | bytes 5406720 | tf_op jit(solution)/shard_map/dot_general | solution.py:24
  74.6 7.2 %fusion.3 = f32[32,3712]{1,0:T(8,128)} fusion(f32[512,3712]{1,0:T(8,128)} %fusion.5, f32[512,3712]{1,0:T(8,128)S(1)} %bitcast.111, s32[512]{0:T(512)S(1)} %bitcast.123, pred[512]{0:T(512)(128)(4,1)S(1)} %compare_reduce_fusion), kind=kOutput, calls=%fused_computation.11 | convolution fusion | flops 731742208 | bytes 15682048 | tf_op jit(solution)/shard_map/dot_general | solution.py:28
  81.8 1.6 %gather_fusion = bf16[29,128,128]{2,1,0:T(8,128)(2,1)} fusion(bf16[7,128,128]{2,1,0:T(8,128)(2,1)S(1)} %copy-done.13, s32[1024]{0:T(1024)S(1)} %pad_clamp_fusion.1), kind=kCustom, calls=%fused_computation | custom fusion | bytes 1900660 | tf_op jit(solution)/shard_map/gather | solution.py:126
  83.5 8.2 %all-gather.3 = f32[4,32,8]{1,2,0:T(8,128)S(1)} all-gather(f32[1,32,8]{1,2,0:T(8,128)S(1)} %copy.55), channel_id=2, replica_groups=mesh['dst'=8,'src'=4] {'src'}, dimensions={0}, use_global_device_ids=true | all-gather | bytes 5120 | tf_op jit(solution)/shard_map/all_gather | solution.py:13
  91.8 8.5 %all-gather.4 = f32[4,32,8]{1,2,0:T(8,128)S(1)} all-gather(f32[1,32,8]{1,2,0:T(8,128)S(1)} %convolution_bitcast_fusion), channel_id=3, replica_groups=mesh['dst'=8,'src'=4] {'src'}, dimensions={0}, use_global_device_ids=true | all-gather | bytes 5120 | tf_op jit(solution)/shard_map/all_gather | solution.py:13
  100.3 15.6 %all-gather.7.cloned.1.call-done = f32[128,3712]{1,0:T(8,128)} async-done(((f32[32,3712]{1,0:T(8,128)}), f32[128,3712]{1,0:T(8,128)}) %all-gather.7.cloned.1.call-update) | async-done | bytes 1900560 | tf_op jit(solution)/shard_map/all_gather | solution.py:13
  117.0 5.9 %while.19 = (s32[]{:T(128)}, f32[32,8]{0,1:T(8,128)S(1)}, f32[32,8]{0,1:T(8,128)S(1)}, f32[32,3712]{1,0:T(8,128)S(1)}, f32[4,32,8]{1,2,0:T(8,128)S(1)}, /*index=...) while((s32[]{:T(128)}, f32[32,8]{0,1:T(8,128)S(1)}, ...), condition=%wide.region_3.4_spmd, body=%wide.region_2.3_spmd.sunk | while | flops 357893 | bytes 3467415 | solution.py:18
  117.3 1.7 %fusion.50 = f32[32,3712]{1,0:T(8,128)S(1)} fusion(f32[4,8,29,128]{3,2,1,0:T(8,128)S(1)} %bitcast.108, f32[32,3712]{1,0:T(8,128)S(1)} %get-tuple-element.268, f32[4,8,29,128]{3,2,1,0:T(8,128)S(1)} %bitcast.109, f32[4,32,3712]{2,1,0:T(8,128)} %get-tuple-element.281, s32[]{:T(128)S(6)} %select_n.137), kind=kLoop, calls=%fused_computation.3.clone.1 | loop fusion | flops 356352 | bytes 2375684 | tf_op jit(solution)/shard_map/while/body/eval_jaxpr/add | solution.py:114
  119.3 1.7 %fusion.50 = f32[32,3712]{1,0:T(8,128)S(1)} fusion(f32[4,8,29,128]{3,2,1,0:T(8,128)S(1)} %bitcast.108, f32[32,3712]{1,0:T(8,128)S(1)} %get-tuple-element.268, f32[4,8,29,128]{3,2,1,0:T(8,128)S(1)} %bitcast.109, f32[4,32,3712]{2,1,0:T(8,128)} %get-tuple-element.281, s32[]{:T(128)S(6)} %select_n.137), kind=kLoop, calls=%fused_computation.3.clone.1 | loop fusion | flops 356352 | bytes 2375684 | tf_op jit(solution)/shard_map/while/body/eval_jaxpr/add | solution.py:114
  121.2 1.7 %fusion.50 = f32[32,3712]{1,0:T(8,128)S(1)} fusion(f32[4,8,29,128]{3,2,1,0:T(8,128)S(1)} %bitcast.108, f32[32,3712]{1,0:T(8,128)S(1)} %get-tuple-element.268, f32[4,8,29,128]{3,2,1,0:T(8,128)S(1)} %bitcast.109, f32[4,32,3712]{2,1,0:T(8,128)} %get-tuple-element.281, s32[]{:T(128)S(6)} %select_n.137), kind=kLoop, calls=%fused_computation.3.clone.1 | loop fusion | flops 356352 | bytes 2375684 | tf_op jit(solution)/shard_map/while/body/eval_jaxpr/add | solution.py:114
  123.2 2.2 %fusion.7 = bf16[8,3712]{1,0:T(8,128)(2,1)} fusion(bf16[29,128,128]{2,1,0:T(8,128)(2,1)} %gather_fusion, f32[32,3712]{1,0:T(8,128)S(1)} %get-tuple-element.182, s32[]{:T(128)S(6)} %select_n.99, f32[8,128]{1,0:T(8,128)S(1)} %tile.112), kind=kOutput, calls=%fused_computation.26 | convolution fusion | flops 7691264 | bytes 1132548 | tf_op jit(solution)/shard_map/acx,cxy->acy/dot_general | solution.py:127
  (102 shorter events, 6.5 us)
Async XLA Ops:
  6.5 29.4 %copy-start = (bf16[896,896]{1,0:T(8,128)(2,1)S(1)}, bf16[896,896]{1,0:T(8,128)(2,1)}, u32[]{:S(2)}) copy-start(bf16[896,896]{1,0:T(8,128)(2,1)} %param.25) | copy-start | bytes 4816900
  6.5 8.9 %copy-start.18 = (bf16[1,512,128]{2,1,0:T(8,128)(2,1)S(1)}, bf16[1,512,128]{2,1,0:T(8,128)(2,1)}, u32[]{:S(2)}) copy-start(bf16[1,512,128]{2,1,0:T(8,128)(2,1)} %param.22) | copy-start | bytes 393220
  8.3 20.6 %all-to-all-start = ((bf16[8,8,3712]{2,1,0:T(8,128)(2,1)}), bf16[8,8,3712]{2,1,0:T(8,128)(2,1)S(1)}, u32[]{:S(2)}, u32[]{:S(2)}) async-start(bf16[8,8,3712]{2,1,0:T(8,128)(2,1)} %stack.2), calls=%async_computation | async-start | bytes 950272 | tf_op jit(solution)/shard_map/all_to_all | solution.py:83
  14.7 101.3 %all-gather.7.cloned.1.call-start = ((), (), s32[]{:S(2)}) async-start(), calls=%async_computation.1 | async-start | bytes 2375680 | tf_op jit(solution)/shard_map/all_gather | solution.py:13
  16.4 4.3 %copy-start.12 = (f32[512,128]{0,1:T(8,128)}, f32[512,128]{0,1:T(8,128)S(1)}, u32[]{:S(2)}) copy-start(f32[512,128]{0,1:T(8,128)S(1)} %fusion.13) | copy-start | bytes 786436
  26.2 1.5 %copy-start.21 = (s32[1,512]{1,0:T(1,128)S(1)}, s32[1,512]{1,0:T(1,128)}, u32[]{:S(2)}) copy-start(s32[1,512]{1,0:T(1,128)} %param.21) | copy-start | bytes 6148
  26.2 1.5 %copy-start.20 = (s32[1,512]{1,0:T(1,128)S(1)}, s32[1,512]{1,0:T(1,128)}, u32[]{:S(2)}) copy-start(s32[1,512]{1,0:T(1,128)} %param.19) | copy-start | bytes 6148
  26.2 1.5 %copy-start.22 = (s32[1,512]{1,0:T(1,128)S(1)}, s32[1,512]{1,0:T(1,128)}, u32[]{:S(2)}) copy-start(s32[1,512]{1,0:T(1,128)} %param.20) | copy-start | bytes 6148
  33.2 2.7 %copy-start.7 = (f32[512,896]{1,0:T(8,128)S(1)}, f32[512,896]{1,0:T(8,128)}, u32[]{:S(2)}) copy-start(f32[512,896]{1,0:T(8,128)} %copy.53) | copy-start | bytes 5505028
  35.9 2.6 %copy-start.4 = (bf16[512,3712]{1,0:T(8,128)(2,1)}, bf16[512,3712]{1,0:T(8,128)(2,1)S(1)}, u32[]{:S(2)}) copy-start(bf16[512,3712]{1,0:T(8,128)(2,1)S(1)} %broadcast_select_fusion) | copy-start | bytes 11403268
  35.9 2.6 %copy-start.23 = (f32[128]{0:T(128)S(1)}, f32[128]{0:T(128)}, u32[]{:S(2)}) copy-start(f32[128]{0:T(128)} %param.30) | copy-start | bytes 1540
  35.9 4.5 %copy-start.19 = (f32[1,8,512]{2,1,0:T(8,128)S(1)}, f32[1,8,512]{2,1,0:T(8,128)}, u32[]{:S(2)}) copy-start(f32[1,8,512]{2,1,0:T(8,128)} %param.23) | copy-start | bytes 49156
  35.9 4.8 %copy-start.1 = (f32[512,768]{1,0:T(8,128)S(1)}, f32[512,768]{1,0:T(8,128)}, u32[]{:S(2)}) copy-start(f32[512,768]{1,0:T(8,128)} %copy.57) | copy-start | bytes 4718596
  40.8 3.7 %copy-start.5 = (bf16[512,3712]{1,0:T(8,128)(2,1)S(1)}, bf16[512,3712]{1,0:T(8,128)(2,1)}, u32[]{:S(2)}) copy-start(bf16[512,3712]{1,0:T(8,128)(2,1)} %copy-done.4) | copy-start | bytes 11403268
  40.8 3.7 %copy-start.11 = (bf16[768,768]{1,0:T(8,128)(2,1)S(1)}, bf16[768,768]{1,0:T(8,128)(2,1)}, u32[]{:S(2)}) copy-start(bf16[768,768]{1,0:T(8,128)(2,1)} %param.27) | copy-start | bytes 3538948
  44.5 2.0 %copy-start.2 = (f32[512,640]{1,0:T(8,128)S(1)}, f32[512,640]{1,0:T(8,128)}, u32[]{:S(2)}) copy-start(f32[512,640]{1,0:T(8,128)} %copy.60) | copy-start | bytes 3932164
  44.5 1.9 %copy-start.16 = (bf16[640,640]{1,0:T(8,128)(2,1)S(1)}, bf16[640,640]{1,0:T(8,128)(2,1)}, u32[]{:S(2)}) copy-start(bf16[640,640]{1,0:T(8,128)(2,1)} %param.28) | copy-start | bytes 2457604
  46.5 1.9 %copy-start.14 = (bf16[640,640]{1,0:T(8,128)(2,1)S(1)}, bf16[640,640]{1,0:T(8,128)(2,1)}, u32[]{:S(2)}) copy-start(bf16[640,640]{1,0:T(8,128)(2,1)} %param.29) | copy-start | bytes 2457604
  63.0 4.2 %copy-start.6 = (bf16[512,3712]{1,0:T(8,128)(2,1)S(1)}, bf16[512,3712]{1,0:T(8,128)(2,1)}, u32[]{:S(2)}) copy-start(bf16[512,3712]{1,0:T(8,128)(2,1)} %copy-done.4) | copy-start | bytes 11403268
  63.0 4.2 %copy-start.8 = (f32[512,768]{1,0:T(8,128)S(1)}, f32[512,768]{1,0:T(8,128)}, u32[]{:S(2)}) copy-start(f32[512,768]{1,0:T(8,128)} %fusion.31) | copy-start | bytes 4718596
  63.1 7.7 %copy-start.10 = (f32[512,640]{1,0:T(8,128)S(1)}, f32[512,640]{1,0:T(8,128)}, u32[]{:S(2)}) copy-start(f32[512,640]{1,0:T(8,128)} %fusion.30) | copy-start | bytes 3932164
  67.3 3.5 %copy-start.3 = (f32[512,640]{1,0:T(8,128)S(1)}, f32[512,640]{1,0:T(8,128)}, u32[]{:S(2)}) copy-start(f32[512,640]{1,0:T(8,128)} %copy.60) | copy-start | bytes 3932164
  67.3 3.5 %copy-start.15 = (bf16[640,640]{1,0:T(8,128)(2,1)S(1)}, bf16[640,640]{1,0:T(8,128)(2,1)}, u32[]{:S(2)}) copy-start(bf16[640,640]{1,0:T(8,128)(2,1)} %param.29) | copy-start | bytes 2457604
  67.3 5.4 %copy-start.17 = (bf16[640,640]{1,0:T(8,128)(2,1)S(1)}, bf16[640,640]{1,0:T(8,128)(2,1)}, u32[]{:S(2)}) copy-start(bf16[640,640]{1,0:T(8,128)(2,1)} %param.28) | copy-start | bytes 2457604
  67.3 7.2 %slice-start = ((s8[7602176]{0:T(1024)(128)(4,1)}), s8[4194304]{0:T(1024)(128)(4,1)S(1)}, s32[]{:S(2)}) async-start(s8[7602176]{0:T(1024)(128)(4,1)} %bitcast.110), calls=%async_computation.2 | async-start | bytes 8388608
  70.7 1.9 %copy-start.9 = (f32[512,640]{1,0:T(8,128)S(1)}, f32[512,640]{1,0:T(8,128)}, u32[]{:S(2)}) copy-start(f32[512,640]{1,0:T(8,128)} %fusion.29) | copy-start | bytes 3932164
  70.7 3.8 %slice-start.1 = ((s8[7602176]{0:T(1024)(128)(4,1)}), s8[3407872]{0:T(1024)(128)(4,1)S(1)}, s32[]{:S(2)}) async-start(s8[7602176]{0:T(1024)(128)(4,1)} %bitcast.110), calls=%async_computation.3 | async-start | bytes 6815744
  74.5 7.3 %copy-start.24 = (s32[29]{0:T(128)S(1)}, s32[29]{0:T(128)}, u32[]{:S(2)}) copy-start(s32[29]{0:T(128)} %constant.134) | copy-start | bytes 352
  74.5 7.3 %copy-start.13 = (bf16[7,128,128]{2,1,0:T(8,128)(2,1)S(1)}, bf16[7,128,128]{2,1,0:T(8,128)(2,1)}, u32[]{:S(2)}) copy-start(bf16[7,128,128]{2,1,0:T(8,128)(2,1)} %param.31) | copy-start | bytes 688132
Sparse Core Ops, SparseCore 0:
  81.9 33.9 all-gather.6
